TPU v7x, 32 devices: a whole 2x2x4 slice. The times are simulated.
32 devices in a mesh: fsdp: 8 (over y, x, core), tp: 4 (over z).
Axes of the slice: x: 2, y: 2, z: 4, core: 2. Of those that a mesh axis runs over, the one named last changes fastest.
Arguments:
- layer_inputs: bfloat16 [1, 2048, 3584], P(None, ('fsdp', 'tp')), may hold values from -6 to 6
- out_grad: bfloat16 [2048, 3584], P(('fsdp', 'tp')), may hold values from -6 to 6
- pre_scale: float32 [1, 3584], replicated, may hold values from 0.1 to 1.9
- post_scale: float32 [1, 3584], replicated, may hold values from 0.1 to 1.9
- gate_weight: bfloat16 [1, 3584, 3584], P(None, 'fsdp', 'tp'), may hold values from -0.09375 to 0.09375
- up_weight: bfloat16 [1, 3584, 3584], P(None, 'fsdp', 'tp'), may hold values from -0.09375 to 0.09375
- down_weight: bfloat16 [1, 3584, 3584], P(None, 'tp', 'fsdp'), may hold values from -0.09375 to 0.09375
Outputs:
- input_grad: bfloat16 [2048, 3584], P(('fsdp', 'tp'))
- gate_grad: bfloat16 [1, 3584, 3584], P(None, 'fsdp', 'tp')
- up_grad: bfloat16 [1, 3584, 3584], P(None, 'fsdp', 'tp')
- down_grad: bfloat16 [1, 3584, 3584], P(None, 'tp', 'fsdp')
All inputs are finite; a program needn't handle non-finite values.
Results may differ from a plain program's by a relative error of at most 0.02.
Values may be sent and summed in bfloat16 or wider, within the bound.
A program may use at most 128 MiB of HBM per device.

v0:
```python
import math

import jax
import jax.numpy as jnp
from jax import lax
from jax.sharding import PartitionSpec as P

epsilon = 1e-06


def own_rows(term, span, axis):
    whole = term(jnp.int32(0), span * lax.axis_size(axis)).astype(jnp.bfloat16)
    return lax.psum_scatter(whole, axis, scatter_dimension=0, tiled=True).astype(jnp.float32)


def rms_factor(values):
    return lax.rsqrt(jnp.mean(values * values, axis=-1, keepdims=True) + epsilon)


def norm_back(delta, normed_in, factor):
    return factor * (delta - normed_in * jnp.mean(delta * normed_in, axis=-1, keepdims=True))


def gelu_tanh(values):
    return jax.nn.gelu(values, approximate=True)


def body(layer_inputs, out_grad, pre_scale, post_scale, gate_weight, up_weight, down_weight):
    tok_rows = out_grad.shape[0]
    layer_count = layer_inputs.shape[0]
    width_rows = gate_weight.shape[1]
    hidden_cols = gate_weight.shape[2]
    grad_scale = 1.0 / math.sqrt(tok_rows * lax.axis_size("fsdp") * lax.axis_size("tp"))
    carried = out_grad.astype(jnp.float32)
    gate_list = [None] * layer_count
    up_list = [None] * layer_count
    down_list = [None] * layer_count
    for layer_id in reversed(range(layer_count)):
        full_gate, full_up, full_down = (
            lax.all_gather(gate_weight[layer_id], "fsdp", axis=0, tiled=True),
            lax.all_gather(up_weight[layer_id], "fsdp", axis=0, tiled=True),
            lax.all_gather(down_weight[layer_id], "fsdp", axis=1, tiled=True),
        )
        layer_in = layer_inputs[layer_id].astype(jnp.float32)
        first_rms = rms_factor(layer_in)
        normed = (layer_in * first_rms * pre_scale[layer_id]).astype(jnp.bfloat16)
        normed_group = lax.all_gather(normed, "tp", axis=0, tiled=True)
        gate_pre = jnp.dot(normed_group, full_gate, preferred_element_type=jnp.float32)
        up_pre = jnp.dot(normed_group, full_up, preferred_element_type=jnp.float32)
        active, gelu_back = jax.vjp(gelu_tanh, gate_pre)
        hidden = (active * up_pre).astype(jnp.bfloat16)
        partial_mlp = jnp.dot(hidden, full_down, preferred_element_type=jnp.float32)
        mlp_out = lax.psum_scatter(
            partial_mlp.astype(jnp.bfloat16), "tp", scatter_dimension=0, tiled=True
        ).astype(jnp.float32)
        mlp_out = lax.optimization_barrier(mlp_out.astype(jnp.bfloat16)).astype(jnp.float32)
        second_rms = rms_factor(mlp_out)
        mlp_grad = norm_back(
            carried * post_scale[layer_id], mlp_out * second_rms, second_rms
        ).astype(jnp.bfloat16)
        grad_group = lax.all_gather(mlp_grad, "tp", axis=0, tiled=True)

        def down_terms(row_start, row_count):
            grad_part = lax.dynamic_slice_in_dim(grad_group, row_start, row_count, 1)
            return jnp.dot(grad_part.T, hidden, preferred_element_type=jnp.float32)

        hidden_grad = jnp.dot(grad_group, full_down.T, preferred_element_type=jnp.float32)
        gate_delta = gelu_back(hidden_grad * up_pre)[0].astype(jnp.bfloat16)
        up_delta = (hidden_grad * active).astype(jnp.bfloat16)

        def width_terms(row_start, row_count):
            normed_part = lax.dynamic_slice_in_dim(normed_group, row_start, row_count, 1)
            return jnp.concatenate(
                [
                    jnp.dot(normed_part.T, gate_delta, preferred_element_type=jnp.float32),
                    jnp.dot(normed_part.T, up_delta, preferred_element_type=jnp.float32),
                ],
                axis=1,
            )

        def weight_terms(row_start, row_count):
            return jnp.concatenate(
                [width_terms(row_start, row_count), down_terms(row_start, row_count)], axis=1
            )

        summed = own_rows(weight_terms, width_rows, "fsdp") * grad_scale
        down_list[layer_id] = summed[:, 2 * hidden_cols :].T.astype(jnp.bfloat16)
        gate_list[layer_id] = summed[:, :hidden_cols].astype(jnp.bfloat16)
        up_list[layer_id] = summed[:, hidden_cols : 2 * hidden_cols].astype(jnp.bfloat16)
        partial_grad = jnp.dot(gate_delta, full_gate.T, preferred_element_type=jnp.float32)
        partial_grad = partial_grad + jnp.dot(
            up_delta, full_up.T, preferred_element_type=jnp.float32
        )
        normed_grad = lax.psum_scatter(
            partial_grad.astype(jnp.bfloat16), "tp", scatter_dimension=0, tiled=True
        ).astype(jnp.float32)
        carried = carried + norm_back(
            normed_grad * pre_scale[layer_id], layer_in * first_rms, first_rms
        )
    return (
        carried.astype(jnp.bfloat16),
        jnp.stack(gate_list),
        jnp.stack(up_list),
        jnp.stack(down_list),
    )


def solution(mesh):
    in_specs = (
        P(None, ("fsdp", "tp"), None),
        P(("fsdp", "tp"), None),
        P(),
        P(),
        P(None, "fsdp", "tp"),
        P(None, "fsdp", "tp"),
        P(None, "tp", "fsdp"),
    )
    out_specs = (
        P(("fsdp", "tp"), None),
        P(None, "fsdp", "tp"),
        P(None, "fsdp", "tp"),
        P(None, "tp", "fsdp"),
    )
    return jax.shard_map(body, mesh=mesh, in_specs=in_specs, out_specs=out_specs, check_vma=False)
```

profile of v0, /device:TPU:0, one launch (start us, length us, event | category | flops | bytes accessed | tf_op | source)
XLA Modules:
  0.0 506.1 jit_solution(11997122378907775372)
XLA Ops:
  7.2 0.0 all-gather.9.cloned.1.call-start
  7.2 1.2 fusion.36
  8.4 0.8 reduce
  9.2 2.0 fusion.32
  11.2 0.0 all-gather.9.cloned.1.call-update
  11.2 0.0 all-gather.13.cloned.1.call-start
  11.2 0.7 all-gather.13.cloned.1.call-update
  11.9 0.0 all-gather.15.cloned.1.call-start
  12.0 0.7 all-gather.15.cloned.1.call-update
  12.7 0.0 all-gather.17.cloned.1.call-start
  12.7 0.5 all-gather.17.cloned.1.call-update
  13.2 0.0 reduce-scatter.6.cloned.1.call-start
  13.3 41.9 %all-gather.9.cloned.1.call-done = bf16[256,3584]{1,0:T(8,128)(2,1)} async-done(((bf16[64,3584]{1,0:T(8,128)(2,1)}), bf16[256,3584]{1,0:T(8,128)(2,1)}) %all-gather.9.cloned.1.call-update) | async-done | bytes 1835024 | tf_op jit(solution)/shard_map/all_gather | solution.py:47
  55.2 46.8 %all-gather.13.cloned.1.call-done = bf16[1,3584,896]{2,1,0:T(8,128)(2,1)} async-done(((bf16[1,448,896]{2,1,0:T(8,128)(2,1)}), bf16[1,3584,896]{2,1,0:T(8,128)(2,1)}) %all-gather.13.cloned.1.call-update) | async-done | bytes 6422544 | tf_op jit(solution)/shard_map/all_gather | solution.py:40
  101.9 6.4 %fusion.10 = f32[256,896]{1,0:T(8,128)} fusion(bf16[256,3584]{1,0:T(8,128)(2,1)} %all-gather.9.cloned.1.call-done, bf16[1,3584,896]{2,1,0:T(8,128)(2,1)} %all-gather.13.cloned.1.call-done), kind=kOutput, calls=%fused_computation.14 | convolution fusion | flops 1644167168 | bytes 9175040 | tf_op jit(solution)/shard_map/dot_general | solution.py:48
  108.3 41.3 %all-gather.15.cloned.1.call-done = bf16[1,3584,896]{2,1,0:T(8,128)(2,1)} async-done(((bf16[1,448,896]{2,1,0:T(8,128)(2,1)}), bf16[1,3584,896]{2,1,0:T(8,128)(2,1)}) %all-gather.15.cloned.1.call-update) | async-done | bytes 6422544 | tf_op jit(solution)/shard_map/all_gather | solution.py:41
  149.6 6.1 %multiply_convert_fusion.2 = (bf16[256,896]{1,0:T(8,128)(2,1)S(1)}, f32[256,896]{1,0:T(8,128)}) fusion(f32[256,896]{1,0:T(8,128)} %fusion.10, bf16[256,3584]{1,0:T(8,128)(2,1)S(1)} %copy-done, bf16[1,3584,896]{2,1,0:T(8,128)(2,1)} %all-gather.15.cloned.1.call-done), kind=kOutput, calls=%fused_computation.56 | convolution fusion | flops 1646460928 | bytes 10551296 | tf_op jit(solution)/shard_map/dot_general | solution.py:49
  155.7 41.4 %all-gather.17.cloned.1.call-done = bf16[1,896,3584]{1,2,0:T(8,128)(2,1)} async-done(((bf16[1,896,448]{1,2,0:T(8,128)(2,1)}), bf16[1,896,3584]{1,2,0:T(8,128)(2,1)}) %all-gather.17.cloned.1.call-update) | async-done | bytes 6422544 | tf_op jit(solution)/shard_map/all_gather | solution.py:42
  197.1 6.2 %fusion.18 = bf16[256,3584]{1,0:T(8,128)(2,1)} fusion(bf16[256,896]{1,0:T(8,128)(2,1)S(1)} %get-tuple-element.17, bf16[1,896,3584]{1,2,0:T(8,128)(2,1)} %all-gather.17.cloned.1.call-done), kind=kOutput, calls=%fused_computation.19 | convolution fusion | flops 1645084672 | bytes 8716288 | tf_op jit(solution)/shard_map/dot_general | solution.py:52
  203.3 0.0 all-gather.11.cloned.1.call-start
  203.4 39.8 %reduce-scatter.6.cloned.1.call-done = bf16[64,3584]{1,0:T(8,128)(2,1)} async-done(((bf16[256,3584]{1,0:T(8,128)(2,1)}), bf16[64,3584]{1,0:T(8,128)(2,1)}) %reduce-scatter.6.cloned.1.call-update) | async-done | bytes 458768 | tf_op jit(solution)/shard_map/reduce_scatter | solution.py:53
  243.2 1.2 fusion.31
  244.5 1.3 fusion.27
  245.8 2.1 fusion.29
  247.9 0.0 reduce-scatter.8.cloned.1.call-start
  247.9 39.9 %all-gather.11.cloned.1.call-done = bf16[256,3584]{1,0:T(8,128)(2,1)} async-done(((bf16[64,3584]{1,0:T(8,128)(2,1)}), bf16[256,3584]{1,0:T(8,128)(2,1)}) %all-gather.11.cloned.1.call-update) | async-done | bytes 1835024 | tf_op jit(solution)/shard_map/all_gather | solution.py:61
  287.9 6.3 %fusion.43 = (bf16[256,896]{1,0:T(8,128)(2,1)S(1)}, bf16[256,896]{1,0:T(8,128)(2,1)S(1)}) fusion(f32[256,896]{1,0:T(8,128)} %fusion.10, f32[256,896]{1,0:T(8,128)} %get-tuple-element.18, bf16[256,3584]{1,0:T(8,128)(2,1)} %all-gather.11.cloned.1.call-done, bf16[1,896,3584]{1,2,0:T(8,128)(2,1)} %all-gather.17.cloned.1.call-done), kind=kOutput, calls=%fused_computation.50 | convolution fusion | flops 1649672192 | bytes 11010048 | tf_op jit(solution)/shard_map/dot_general | solution.py:67
  294.2 5.1 %fusion.4 = f32[256,3584]{1,0:T(8,128)S(1)} fusion(bf16[256,896]{1,0:T(8,128)(2,1)S(1)} %get-tuple-element.16, bf16[1,3584,896]{2,1,0:T(8,128)(2,1)} %all-gather.15.cloned.1.call-done), kind=kOutput, calls=%fused_computation.8 | convolution fusion | flops 1644167168 | bytes 10551296 | tf_op jit(solution)/shard_map/dot_general | solution.py:91
  299.3 6.1 %fusion.15 = bf16[256,3584]{1,0:T(8,128)(2,1)} fusion(f32[256,3584]{1,0:T(8,128)S(1)} %fusion.4, bf16[256,896]{1,0:T(8,128)(2,1)S(1)} %get-tuple-element.15, bf16[1,3584,896]{2,1,0:T(8,128)(2,1)} %all-gather.13.cloned.1.call-done), kind=kOutput, calls=%fused_computation.18 | convolution fusion | flops 1646002176 | bytes 12386304 | tf_op jit(solution)/shard_map/dot_general | solution.py:90
  305.4 0.0 reduce-scatter.8.cloned.1.call-update
  305.5 0.2 reduce-scatter.10.cloned.1.call-start
  305.7 3.4 convolution_convert_fusion
  309.1 1.9 convolution_convert_fusion.2
  311.0 1.9 convolution_convert_fusion.1
  312.9 26.3 %pad_maximum_fusion = bf16[3584,2688]{0,1:T(8,128)(2,1)} fusion(bf16[3584,896]{0,1:T(8,128)(2,1)S(1)} %convolution_convert_fusion, bf16[3584,896]{0,1:T(8,128)(2,1)S(1)} %convolution_convert_fusion.1, bf16[3584,896]{0,1:T(8,128)(2,1)S(1)} %convolution_convert_fusion.2), kind=kLoop, calls=%fused_computation | loop fusion | flops 57802752 | bytes 38535168 | tf_op jit(solution)/shard_map/concatenate | solution.py:82
  339.2 25.0 %copy.17 = bf16[3584,2688]{1,0:T(8,128)(2,1)} copy(bf16[3584,2688]{0,1:T(8,128)(2,1)} %pad_maximum_fusion) | data formatting | bytes 38535168
  364.2 0.0 reduce-scatter.10.cloned.1.call-update
  364.2 0.0 reduce-scatter.8.cloned.1.call-done
  364.2 1.0 copy-done.1
  365.2 1.3 fusion.33
  366.5 2.1 fusion.30
  368.6 122.9 %reduce-scatter.10.cloned.1.call-done = bf16[448,2688]{1,0:T(8,128)(2,1)} async-done(((bf16[3584,2688]{1,0:T(8,128)(2,1)}), bf16[448,2688]{1,0:T(8,128)(2,1)}) %reduce-scatter.10.cloned.1.call-update) | async-done | bytes 2408464
  491.5 3.2 copy.18
  494.8 0.6 multiply_convert_fusion
  495.3 0.2 slice_bitcast_fusion
  495.5 1.2 copy.16
  496.8 1.2 copy.15
  498.0 1.2 copy.14
  (18 shorter events, 0.1 us)
Async XLA Ops:
  7.2 48.0 %all-gather.9.cloned.1.call-start = ((), (), s32[]{:S(2)}) async-start(), calls=%async_computation.3 | async-start | bytes 2293760 | tf_op jit(solution)/shard_map/all_gather | solution.py:47
  11.2 90.8 %all-gather.13.cloned.1.call-start = ((), (), s32[]{:S(2)}) async-start(), calls=%async_computation.7 | async-start | bytes 7225344 | tf_op jit(solution)/shard_map/all_gather | solution.py:40
  11.9 137.7 %all-gather.15.cloned.1.call-start = ((), (), s32[]{:S(2)}) async-start(), calls=%async_computation.8 | async-start | bytes 7225344 | tf_op jit(solution)/shard_map/all_gather | solution.py:41
  12.7 184.4 %all-gather.17.cloned.1.call-start = ((), (), s32[]{:S(2)}) async-start(), calls=%async_computation.9 | async-start | bytes 7225344 | tf_op jit(solution)/shard_map/all_gather | solution.py:42
  13.2 230.0 %reduce-scatter.6.cloned.1.call-start = ((), (), s32[]{:S(2)}) async-start(), calls=%async_computation.4 | async-start | bytes 2293760 | tf_op jit(solution)/shard_map/reduce_scatter | solution.py:53
  55.2 94.4 %copy-start = (bf16[256,3584]{1,0:T(8,128)(2,1)S(1)}, bf16[256,3584]{1,0:T(8,128)(2,1)}, u32[]{:S(2)}) copy-start(bf16[256,3584]{1,0:T(8,128)(2,1)} %all-gather.9.cloned.1.call-done) | copy-start | bytes 5505028
  155.7 47.7 %copy-start.5 = (f32[1,3584]{1,0:T(1,128)S(1)}, f32[1,3584]{1,0:T(1,128)}, u32[]{:S(2)}) copy-start(f32[1,3584]{1,0:T(1,128)} %param.10) | copy-start | bytes 43012
  155.7 88.8 %copy-start.2 = (bf16[64,3584]{1,0:T(8,128)(2,1)S(1)}, bf16[64,3584]{1,0:T(8,128)(2,1)}, u32[]{:S(2)}) copy-start(bf16[64,3584]{1,0:T(8,128)(2,1)} %param.8) | copy-start | bytes 1376260
  203.3 84.6 %all-gather.11.cloned.1.call-start = ((), (), s32[]{:S(2)}) async-start(), calls=%async_computation.5 | async-start | bytes 2293760 | tf_op jit(solution)/shard_map/all_gather | solution.py:61
  247.9 116.3 %reduce-scatter.8.cloned.1.call-start = ((), (), s32[]{:S(2)}) async-start(), calls=%async_computation.6 | async-start | bytes 2293760 | tf_op jit(solution)/shard_map/reduce_scatter | solution.py:94
  294.2 5.1 %copy-start.3 = (bf16[256,896]{1,0:T(8,128)(2,1)}, bf16[256,896]{1,0:T(8,128)(2,1)S(1)}, u32[]{:S(2)}) copy-start(bf16[256,896]{1,0:T(8,128)(2,1)S(1)} %get-tuple-element.16) | copy-start | bytes 1376260
  305.5 186.1 %reduce-scatter.10.cloned.1.call-start = ((), (), s32[]{:S(2)}) async-start(), calls=%async_computation.10 | async-start | bytes 21676032
  309.1 1.9 copy-start.4
  364.2 1.0 copy-start.1
Sparse Core Ops, SparseCore 0:
  11.3 43.8 all-gather.8
  57.0 44.8 all-gather.12
  103.8 45.7 all-gather.14
  151.3 45.7 all-gather.16
  203.4 39.7 reduce-scatter.5
  248.0 39.8 all-gather.10
  305.6 38.9 reduce-scatter.7
  364.3 127.1 reduce-scatter.9
where the time goes:
time: 507 us; the launch traced here: 506 us
  waiting for transfers between devices  376 us (74%)
  matrix products  43.3 us (9%)
  other arithmetic  38.9 us (8%)
  local copies, waits for them, and re-layouts  33.1 us (7%)
  between operations  14.3 us (3%)
    unnamed x9, waiting for transfers between devices  125 us
    all_gather x1, waiting for transfers between devices, body(): lax.all_gather(gate_weight[layer_id], 'fsdp', axis=0, tiled=True)  46.8 us
    all_gather x1, waiting for transfers between devices, body(): normed_group = lax.all_gather(normed, 'tp', axis=0, tiled=True)  41.9 us
    all_gather x1, waiting for transfers between devices, body(): lax.all_gather(down_weight[layer_id], 'fsdp', axis=1, tiled=True)  41.4 us
    all_gather x1, waiting for transfers between devices, body(): lax.all_gather(up_weight[layer_id], 'fsdp', axis=0, tiled=True)  41.3 us
    all_gather x1, waiting for transfers between devices, body(): grad_group = lax.all_gather(mlp_grad, 'tp', axis=0, tiled=True)  39.9 us
    reduce_scatter x1, waiting for transfers between devices, body(): lax.psum_scatter(partial_mlp.astype(jnp.bfloat16), 'tp', scatter_dimensio...  39.8 us
    unnamed x17, local copies, waits for them, and re-layouts  32.9 us
  transfers between devices with their start and end apart: 8, of which 7 were waited for; matrix products, arithmetic and copies ran while one was open for 15% of the time, Pallas kernels for 0%

commit v1 on v0

v1 whole, which is shorter than its diff:
```python
import functools
import math

import jax
import jax.numpy as jnp
from jax import lax
from jax.experimental import pallas as pl
from jax.experimental.pallas import tpu as pltpu
from jax.sharding import PartitionSpec as P

epsilon = 1e-06
MESH = pl.DeviceIdType.MESH
VMEM_LIMIT = 60 * 1024 * 1024


def rms_factor(values):
    return lax.rsqrt(jnp.mean(values * values, axis=-1, keepdims=True) + epsilon)


def norm_back(delta, normed_in, factor):
    return factor * (delta - normed_in * jnp.mean(delta * normed_in, axis=-1, keepdims=True))


def gelu_tanh(values):
    return jax.nn.gelu(values, approximate=True)


def place(outer):
    me = lax.axis_index("fsdp")
    return me // 4, (me // 2) % 2, me % 2


def index_of(a, b, c):
    return (a * 2 + b) * 2 + c


def remote(src, dst, send_sem, recv_sem, target):
    return pltpu.make_async_remote_copy(
        src_ref=src,
        dst_ref=dst,
        send_sem=send_sem,
        recv_sem=recv_sem,
        device_id={"fsdp": target},
        device_id_type=MESH,
    )


def greet(outer, a, b, c):
    barrier = pltpu.get_barrier_semaphore()
    targets = [index_of(a, b, 1 - c), index_of(a, 1 - b, c)]
    targets += [index_of((a + j) % outer, b, c) for j in range(1, outer)]
    for target in targets:
        pl.semaphore_signal(barrier, inc=1, device_id={"fsdp": target}, device_id_type=MESH)
    pl.semaphore_wait(barrier, len(targets))


def gather_kernel(outer, count, *refs):
    ins, outs = refs[:count], refs[count : 2 * count]
    bounce, local_sem, recv_sem, link_sem, pair_sem = refs[2 * count :]
    a, b, c = place(outer)
    me = index_of(a, b, c)
    partner = index_of(a, b, 1 - c)
    across = index_of(a, 1 - b, c)
    along = [index_of((a + j) % outer, b, c) for j in range(1, outer)]
    diagonal = [index_of((a + j) % outer, 1 - b, c) for j in range(1, outer)]
    greet(outer, a, b, c)

    def push(w, src, slot, sem, target):
        return remote(src, outs[w].at[slot], sem, recv_sem.at[w, slot], target)

    def arrived(w, slot):
        spot = outs[w].at[slot]
        remote(spot, spot, pair_sem.at[w, 0], recv_sem.at[w, slot], partner).wait_recv()

    sent = []
    for w in range(count):
        own = [push(w, ins[w], me, link_sem.at[w, 0], across)]
        own += [push(w, ins[w], me, link_sem.at[w, 1 + j], t) for j, t in enumerate(along)]
        own.append(push(w, ins[w], me, pair_sem.at[w, 0], partner))
        for copy in own:
            copy.start()
        sent += own
    inward = [pltpu.make_async_copy(ins[w], bounce.at[w], local_sem.at[w]) for w in range(count)]
    outward = [
        pltpu.make_async_copy(bounce.at[w], outs[w].at[me], local_sem.at[w]) for w in range(count)
    ]
    for w in range(count):
        inward[w].start()
    for w in range(count):
        inward[w].wait()
        outward[w].start()
    forwards = []
    for w in range(count):
        arrived(w, across)
        copy = push(w, outs[w].at[across], across, pair_sem.at[w, 1], partner)
        copy.start()
        sent.append(copy)
        for j, target in enumerate(along):
            copy = push(w, outs[w].at[across], across, link_sem.at[w, outer + j], target)
            pl.when(c == 0)(copy.start)
            forwards.append((0, copy))
        for j, slot in enumerate(along):
            arrived(w, slot)
            copy = push(w, outs[w].at[slot], slot, link_sem.at[w, outer + j], across)
            pl.when(c == 1)(copy.start)
            forwards.append((1, copy))
            copy = push(w, outs[w].at[slot], slot, pair_sem.at[w, 2 + j], partner)
            copy.start()
            sent.append(copy)
    for w in range(count):
        for j, slot in enumerate(diagonal):
            arrived(w, slot)
            copy = push(w, outs[w].at[slot], slot, pair_sem.at[w, 1 + outer + j], partner)
            copy.start()
            sent.append(copy)
    for w in range(count):
        for chip in range(2 * outer):
            arrived(w, chip * 2 + 1 - c)
        outward[w].wait()
    for copy in sent:
        copy.wait_send()
    for core, copy in forwards:
        pl.when(c == core)(copy.wait_send)


def gather_blocks(blocks, parts):
    outer, count = parts // 4, len(blocks)
    rows, columns = blocks[0].shape
    dtype = blocks[0].dtype
    size = rows * columns * dtype.itemsize * count
    outs = pl.pallas_call(
        functools.partial(gather_kernel, outer, count),
        out_shape=[jax.ShapeDtypeStruct((parts, rows, columns), dtype)] * count,
        in_specs=[pl.BlockSpec(memory_space=pl.ANY)] * count,
        out_specs=[pl.BlockSpec(memory_space=pl.ANY)] * count,
        scratch_shapes=[
            pltpu.VMEM((count, rows, columns), dtype),
            pltpu.SemaphoreType.DMA((count,)),
            pltpu.SemaphoreType.DMA((count, parts)),
            pltpu.SemaphoreType.DMA((count, 2 * outer - 1)),
            pltpu.SemaphoreType.DMA((count, 2 * outer)),
        ],
        compiler_params=pltpu.CompilerParams(
            collective_id=0, has_side_effects=True, vmem_limit_bytes=8 * 1024 * 1024
        ),
        cost_estimate=pl.CostEstimate(
            flops=200_000_000, bytes_accessed=2 * parts * size, transcendentals=0
        ),
    )(*blocks)
    return [out.reshape(parts * rows, columns) for out in outs]


def scatter_kernel(outer, scale, left, right, out, psend, precv, total, first, second,
                   psend_sem, precv_sem, send1, recv1, send2, recv2):
    count = right.shape[0]
    rows = out.shape[1]
    half = rows // 2
    chips = 2 * outer
    a, b, c = place(outer)
    partner = index_of(a, b, 1 - c)
    across = index_of(a, 1 - b, c)
    greet(outer, a, b, c)

    def spot(p):
        return (p % outer + 1) % outer, 1 - p // outer

    def term(p, w, core, h):
        da, db = spot(p)
        owner = index_of((a + da) % outer, (b + db) % 2, core)
        start = pl.multiple_of(owner * rows + h * half, 16)
        return jnp.dot(
            left[w // 2, pl.ds(start, half), :], right[w], preferred_element_type=jnp.float32
        )

    def part(h):
        return pl.ds(pl.multiple_of(h * half, 16), half)

    def to_partner(p, w):
        return remote(psend.at[p, w], precv.at[p, w], psend_sem.at[p, w], precv_sem.at[p, w], partner)

    def hop1_across(p, w):
        da, _ = spot(p)
        return remote(total.at[p, w], first.at[da, w], send1.at[p, w], recv1.at[da, w], across)

    def hop1_along(p, w):
        da, db = spot(p)
        slot = (da - 1) * 2 + db
        target = index_of((a + da) % outer, b, c)
        return remote(total.at[p, w], first.at[slot, w], send1.at[p, w], recv1.at[slot, w], target)

    def first_arrived(slot, w):
        remote(first.at[slot, w], first.at[slot, w], send1.at[0, w], recv1.at[slot, w],
               across).wait_recv()

    def second_arrived(slot, w):
        remote(second.at[slot, w], second.at[slot, w], send2.at[0, w], recv2.at[slot, w],
               across).wait_recv()

    @pl.loop(0, chips * count)
    def _(i):
        p, w = i // count, i % count

        @pl.loop(0, 2)
        def _(h):
            psend[p, w, part(h), :] = term(p, w, 1 - c, h).astype(psend.dtype)

        to_partner(p, w).start()

    @pl.loop(0, chips * count)
    def _(i):
        p, w = i // count, i % count
        da, db = spot(p)
        to_partner(p, w).wait_recv()

        @pl.loop(0, 2)
        def _(h):
            total[p, w, part(h), :] = (
                term(p, w, c, h) + precv[p, w, part(h), :].astype(jnp.float32)
            ).astype(total.dtype)

        @pl.when((c == 0) & (db == 1))
        def _():
            hop1_across(p, w).start()

        @pl.when((c == 1) & (da != 0))
        def _():
            hop1_along(p, w).start()

    spots = [((p % outer + 1) % outer, 1 - p // outer) for p in range(chips)]
    where = {key: p for p, key in enumerate(spots)}

    def hop2(p, slot, w, target):
        return remote(total.at[p, w], second.at[slot, w], send2.at[slot, w], recv2.at[slot, w], target)

    def hop2_along(da, w):
        return hop2(where[da, 0], da - 1, w, index_of((a + da) % outer, b, c))

    def hop2_across(w):
        return hop2(where[0, 1], 0, w, across)

    def summed(p, w, slots, h):
        value = total[p, w, part(h), :].astype(jnp.float32)
        for ref, slot in slots:
            value = value + ref[slot, w, part(h), :].astype(jnp.float32)
        return value

    def settle(p, w, slots):
        @pl.loop(0, 2)
        def _(h):
            total[p, w, part(h), :] = summed(p, w, slots, h).astype(total.dtype)

    def finish(w, slots):
        @pl.loop(0, 2)
        def _(h):
            out[w, part(h), :] = (summed(where[0, 0], w, slots, h) * scale).astype(out.dtype)

    @pl.when(c == 0)
    def _():
        @pl.loop(0, count)
        def _(w):
            for da in range(1, outer):
                first_arrived(da, w)
                settle(where[da, 0], w, [(first, da)])
                hop2_along(da, w).start()

        @pl.loop(0, count)
        def _(w):
            first_arrived(0, w)
            for da in range(1, outer):
                second_arrived(da - 1, w)
            finish(w, [(first, 0)] + [(second, da - 1) for da in range(1, outer)])
            for da in range(outer):
                hop1_across(where[da, 1], w).wait_send()
            for da in range(1, outer):
                hop2_along(da, w).wait_send()

    @pl.when(c == 1)
    def _():
        @pl.loop(0, count)
        def _(w):
            slots = [(da - 1) * 2 + 1 for da in range(1, outer)]
            for slot in slots:
                first_arrived(slot, w)
            settle(where[0, 1], w, [(first, slot) for slot in slots])
            hop2_across(w).start()

        @pl.loop(0, count)
        def _(w):
            slots = [(da - 1) * 2 for da in range(1, outer)]
            for slot in slots:
                first_arrived(slot, w)
            second_arrived(0, w)
            finish(w, [(first, slot) for slot in slots] + [(second, 0)])
            for da in range(1, outer):
                for db in range(2):
                    hop1_along(where[da, db], w).wait_send()
            hop2_across(w).wait_send()

    @pl.loop(0, chips * count)
    def _(i):
        to_partner(i // count, i % count).wait_send()


def scatter_products(left, right, parts, scale):
    outer, count = parts // 4, right.shape[0]
    rows, columns = left.shape[1] // parts, right.shape[2]
    chips = 2 * outer
    hop1 = max(outer, 2 * (outer - 1))
    hop2 = max(outer - 1, 1)
    block = (count, rows, columns)
    dma = pltpu.SemaphoreType.DMA
    return pl.pallas_call(
        functools.partial(scatter_kernel, outer, scale),
        out_shape=jax.ShapeDtypeStruct(block, jnp.bfloat16),
        in_specs=[pl.BlockSpec(memory_space=pltpu.VMEM)] * 2,
        out_specs=pl.BlockSpec(memory_space=pltpu.VMEM),
        scratch_shapes=[
            pltpu.VMEM((chips,) + block, jnp.bfloat16),
            pltpu.VMEM((chips,) + block, jnp.bfloat16),
            pltpu.VMEM((chips,) + block, jnp.bfloat16),
            pltpu.VMEM((hop1,) + block, jnp.bfloat16),
            pltpu.VMEM((hop2,) + block, jnp.bfloat16),
            dma((chips, count)),
            dma((chips, count)),
            dma((chips, count)),
            dma((hop1, count)),
            dma((hop2, count)),
            dma((hop2, count)),
        ],
        compiler_params=pltpu.CompilerParams(
            collective_id=1, has_side_effects=True, vmem_limit_bytes=VMEM_LIMIT
        ),
        cost_estimate=pl.CostEstimate(
            flops=2 * left.shape[1] * left.shape[2] * columns * count,
            bytes_accessed=2 * chips * count * rows * columns * 2,
            transcendentals=0,
        ),
    )(left, right)


def body(parts, layer_inputs, out_grad, pre_scale, post_scale, gate_weight, up_weight, down_weight):
    tok_rows = out_grad.shape[0]
    layer_count = layer_inputs.shape[0]
    grad_scale = 1.0 / math.sqrt(tok_rows * lax.axis_size("fsdp") * lax.axis_size("tp"))
    carried = out_grad.astype(jnp.float32)
    gate_list = [None] * layer_count
    up_list = [None] * layer_count
    down_list = [None] * layer_count

    def nt(x, y):
        return lax.dot_general(x, y, (((1,), (1,)), ((), ())), preferred_element_type=jnp.float32)

    for layer_id in reversed(range(layer_count)):
        layer_in = layer_inputs[layer_id].astype(jnp.float32)
        first_rms = rms_factor(layer_in)
        normed = (layer_in * first_rms * pre_scale[layer_id]).astype(jnp.bfloat16)
        normed_group = lax.all_gather(normed, "tp", axis=0, tiled=True)
        full_gate, full_up, full_down = gather_blocks(
            [gate_weight[layer_id], up_weight[layer_id], down_weight[layer_id].T], parts
        )
        gate_pre = jnp.dot(normed_group, full_gate, preferred_element_type=jnp.float32)
        up_pre = jnp.dot(normed_group, full_up, preferred_element_type=jnp.float32)
        active, gelu_back = jax.vjp(gelu_tanh, gate_pre)
        hidden = (active * up_pre).astype(jnp.bfloat16)
        partial_mlp = nt(hidden, full_down)
        mlp_out = lax.psum_scatter(
            partial_mlp.astype(jnp.bfloat16), "tp", scatter_dimension=0, tiled=True
        ).astype(jnp.float32)
        mlp_out = lax.optimization_barrier(mlp_out.astype(jnp.bfloat16)).astype(jnp.float32)
        second_rms = rms_factor(mlp_out)
        mlp_grad = norm_back(
            carried * post_scale[layer_id], mlp_out * second_rms, second_rms
        ).astype(jnp.bfloat16)
        grad_group = lax.all_gather(mlp_grad, "tp", axis=0, tiled=True)
        hidden_grad = jnp.dot(grad_group, full_down, preferred_element_type=jnp.float32)
        gate_delta = gelu_back(hidden_grad * up_pre)[0].astype(jnp.bfloat16)
        up_delta = (hidden_grad * active).astype(jnp.bfloat16)
        partial_grad = nt(gate_delta, full_gate) + nt(up_delta, full_up)
        normed_grad = lax.psum_scatter(
            partial_grad.astype(jnp.bfloat16), "tp", scatter_dimension=0, tiled=True
        ).astype(jnp.float32)
        summed = scatter_products(
            jnp.stack([normed_group.T, grad_group.T]),
            jnp.stack([gate_delta, up_delta, hidden]),
            parts,
            grad_scale,
        )
        gate_list[layer_id] = summed[0]
        up_list[layer_id] = summed[1]
        down_list[layer_id] = summed[2].T
        carried = carried + norm_back(
            normed_grad * pre_scale[layer_id], layer_in * first_rms, first_rms
        )
    return (
        carried.astype(jnp.bfloat16),
        jnp.stack(gate_list),
        jnp.stack(up_list),
        jnp.stack(down_list),
    )


def solution(mesh):
    in_specs = (
        P(None, ("fsdp", "tp"), None),
        P(("fsdp", "tp"), None),
        P(),
        P(),
        P(None, "fsdp", "tp"),
        P(None, "fsdp", "tp"),
        P(None, "tp", "fsdp"),
    )
    out_specs = (
        P(("fsdp", "tp"), None),
        P(None, "fsdp", "tp"),
        P(None, "fsdp", "tp"),
        P(None, "tp", "fsdp"),
    )
    step = functools.partial(body, mesh.shape["fsdp"])
    return jax.shard_map(step, mesh=mesh, in_specs=in_specs, out_specs=out_specs, check_vma=False)
```

time: 507 us -> 339 us (0.67)
  waiting for transfers between devices: 376 us -> 79.9 us
  Pallas kernels: 0 us -> 179 us
  other arithmetic: 38.9 us -> 13.7 us
  matrix products: 43.3 us -> 26.9 us
  local copies, waits for them, and re-layouts: 33.1 us -> 23.9 us
    pallas_call x0 -> x2, Pallas kernels: none -> 179 us  [the longest x1 94.4 us: scatter_products(): pl.pallas_call(functools.partial(scatter_kernel, outer, scale), out_shape...]
    all_gather x3 -> x0, waiting for transfers between devices: 129 us -> none  [the longest x1 46.8 us: body(): lax.all_gather(gate_weight[layer_id], 'fsdp', axis=0, tiled=True)]
    unnamed x9 -> x5, waiting for transfers between devices: 125 us -> 40.2 us
    all_gather x1, waiting for transfers between devices: 41.9 us -> 0.01 us  [body(): normed_group = lax.all_gather(normed, 'tp', axis=0, tiled=True)]
    reduce_scatter x1 -> x0, waiting for transfers between devices: 39.8 us -> none  [body(): lax.psum_scatter(partial_mlp.astype(jnp.bfloat16), 'tp', scatter_dimensio...]
    concatenate x1 -> x0, other arithmetic: 26.3 us -> none  [weight_terms(): jnp.concatenate([width_terms(row_start, row_count), down_terms(row_start,...]
    unnamed x17 -> x37, local copies, waits for them, and re-layouts: 32.9 us -> 13.8 us
    dot_general x7 -> x4, matrix products: 30.8 us -> 18.3 us  [the longest x3 11.8 us: nt(): lax.dot_general(x, y, (((1,), (1,)), ((), ())), preferred_element_type=jn...]
  transfers between devices with their start and end apart: 8 -> 4, of which waited for: 7 -> 2; matrix products, arithmetic and copies ran while one was open for 15% -> 4% of each run, Pallas kernels for 0% -> 53%
where the time goes in v1:
time: 339 us; the launch traced here: 338 us
  Pallas kernels  179 us (53%)
  waiting for transfers between devices  79.9 us (24%)
  matrix products  26.9 us (8%)
  local copies, waits for them, and re-layouts  23.9 us (7%)
  between operations  14 us (4%)
  other arithmetic  13.7 us (4%)
    pallas_call x1, Pallas kernels, scatter_products(): pl.pallas_call(functools.partial(scatter_kernel, outer, scale), out_shape...  94.4 us
    pallas_call x1, Pallas kernels, gather_blocks(): pl.pallas_call(functools.partial(gather_kernel, outer, count), out_shape=...  84.7 us
    unnamed x5, waiting for transfers between devices  40.2 us
    all_gather x1, waiting for transfers between devices, body(): grad_group = lax.all_gather(mlp_grad, 'tp', axis=0, tiled=True)  39.7 us
    unnamed x37, local copies, waits for them, and re-layouts  13.8 us
    dot_general x3, matrix products, nt(): lax.dot_general(x, y, (((1,), (1,)), ((), ())), preferred_element_type=jn...  11.8 us
  transfers between devices with their start and end apart: 4, of which 2 were waited for; matrix products, arithmetic and copies ran while one was open for 4% of the time, Pallas kernels for 53%

profile of v1, /device:TPU:0, one launch (start us, length us, event | category | flops | bytes accessed | tf_op | source)
XLA Modules:
  0.0 337.9 jit_solution(11249102049356271273)
XLA Ops:
  7.2 0.0 all-gather.3.cloned.1.call-start
  7.2 1.2 fusion.16
  8.4 0.8 reduce
  9.2 2.0 fusion.12
  11.2 0.0 all-gather.3.cloned.1.call-update
  11.2 0.0 reduce-scatter.7.cloned.1.call-start
  11.2 0.0 copy-start.2
  11.2 1.1 copy-done.2
  12.4 1.1 copy-done.3
  13.5 1.1 copy-done.4
  14.7 84.7 %shard_map.102 = (bf16[8,448,896]{2,1,0:T(8,128)(2,1)S(1)}, bf16[8,448,896]{2,1,0:T(8,128)(2,1)S(1)}, bf16[8,448,896]{2,1,0:T(8,128)(2,1)S(1)}) custom-call(bf16[448,896]{1,0:T(8,128)(2,1)S(1)} %bitcast.47, bf16[448,896]{1,0:T(8,128)(2,1)S(1)} %bitcast.48, bf16[448,896]{1,0:T(8,128)(2,1)S(1)} %bitcast.49), custom_call_target="tpu_custom_call" | custom-call | flops 200000000 | bytes 38535168 | tf_op jit(solution)/shard_map/pallas_call | solution.py:131
  99.4 0.0 copy-start
  99.4 2.7 copy-done
  102.1 2.7 copy-done.5
  104.8 2.6 copy-done.6
  107.4 5.6 %fusion.24 = f32[256,896]{1,0:T(8,128)S(1)} fusion(bf16[256,3584]{1,0:T(8,128)(2,1)} %all-gather.3.cloned.1.call-done, bf16[3584,896]{1,0:T(8,128)(2,1)} %bitcast.50), kind=kOutput, calls=%fused_computation.45 | convolution fusion | flops 1644167168 | bytes 9175040 | tf_op jit(solution)/shard_map/dot_general | solution.py:361
  113.0 0.0 copy-start.15
  113.0 0.0 copy-done.1
  113.0 0.1 copy-done.11
  113.1 3.0 multiply_convert_fusion.1
  116.1 0.8 copy-done.12
  116.9 0.0 copy-done.7
  116.9 3.4 %convolution_convert_fusion = bf16[256,3584]{1,0:T(8,128)(2,1)} fusion(bf16[256,896]{1,0:T(8,128)(2,1)S(1)} %get-tuple-element.19, bf16[3584,896]{1,0:T(8,128)(2,1)S(1)} %bitcast.53), kind=kOutput, calls=%fused_computation.2 | convolution fusion | flops 1645084672 | bytes 8716288 | tf_op jit(solution)/shard_map/dot_general | solution.py:351
  120.3 0.0 reduce-scatter.7.cloned.1.call-update
  120.3 0.0 all-gather.5.cloned.1.call-start
  120.4 40.1 %reduce-scatter.7.cloned.1.call-done = bf16[64,3584]{1,0:T(8,128)(2,1)} async-done(((bf16[256,3584]{1,0:T(8,128)(2,1)}), bf16[64,3584]{1,0:T(8,128)(2,1)}) %reduce-scatter.7.cloned.1.call-update) | async-done | bytes 458768
  160.6 1.4 copy.24
  162.0 0.3 copy.18
  162.3 0.2 fusion.11
  162.5 0.3 fusion.7
  162.9 1.0 fusion.9
  163.9 0.0 all-gather.5.cloned.1.call-update
  163.9 0.2 reduce-scatter.9.cloned.1.call-start
  164.2 39.7 %all-gather.5.cloned.1.call-done = bf16[256,3584]{1,0:T(8,128)(2,1)} async-done(((bf16[64,3584]{1,0:T(8,128)(2,1)}), bf16[256,3584]{1,0:T(8,128)(2,1)}) %all-gather.5.cloned.1.call-update) | async-done | bytes 1835024 | tf_op jit(solution)/shard_map/all_gather | solution.py:374
  203.9 6.5 %multiply_convert_fusion = (bf16[256,896]{1,0:T(8,128)(2,1)S(1)}, bf16[256,896]{1,0:T(8,128)(2,1)S(1)}) fusion(f32[256,896]{1,0:T(8,128)} %copy-done.15, f32[256,896]{1,0:T(8,128)} %get-tuple-element.20, bf16[256,3584]{1,0:T(8,128)(2,1)} %all-gather.5.cloned.1.call-done, bf16[3584,896]{1,0:T(8,128)(2,1)} %bitcast.52), kind=kOutput, calls=%fused_computation.37 | convolution fusion | flops 1649672192 | bytes 11010048 | tf_op jit(solution)/shard_map/dot_general | solution.py:375
  210.4 0.0 copy-start.13
  210.4 5.1 %fusion.25 = f32[256,3584]{1,0:T(8,128)S(1)} fusion(bf16[256,896]{1,0:T(8,128)(2,1)S(1)} %get-tuple-element.18, bf16[3584,896]{1,0:T(8,128)(2,1)} %bitcast.51), kind=kOutput, calls=%fused_computation.46 | convolution fusion | flops 1644167168 | bytes 10551296 | tf_op jit(solution)/shard_map/dot_general | solution.py:351
  215.6 3.3 fusion
  218.9 0.0 reduce-scatter.9.cloned.1.call-update
  218.9 2.9 copy.21
  221.8 3.8 %copy.22 = bf16[256,3584]{0,1:T(8,128)(2,1)} copy(bf16[256,3584]{1,0:T(8,128)(2,1)} %all-gather.5.cloned.1.call-done) | data formatting | bytes 3670016 | tf_op jit(solution)/shard_map/all_gather | solution.py:374
  225.6 2.6 pad_maximum_fusion.1.right
  228.2 2.1 pad_maximum_fusion.left
  230.4 94.4 %shard_map.103 = bf16[3,448,896]{2,1,0:T(8,128)(2,1)} custom-call(bf16[2,3584,256]{2,1,0:T(8,128)(2,1)} %pad_maximum_fusion.left, bf16[3,256,896]{2,1,0:T(8,128)(2,1)} %pad_maximum_fusion.1.right), custom_call_target="tpu_custom_call" | custom-call | flops 4932501504 | bytes 19267584 | tf_op jit(solution)/shard_map/pallas_call | solution.py:312
  324.7 0.0 copy-start.9
  324.7 3.2 slice_bitcast_fusion
  327.9 1.3 fusion.13
  329.2 2.1 fusion.10
  (29 shorter events, 0.1 us)
Async XLA Ops:
  7.2 100.2 %all-gather.3.cloned.1.call-start = ((), (), s32[]{:S(2)}) async-start(), calls=%async_computation.2 | async-start | bytes 2293760 | tf_op jit(solution)/shard_map/all_gather | solution.py:357
  11.2 149.4 %reduce-scatter.7.cloned.1.call-start = ((), (), s32[]{:S(2)}) async-start(), calls=%async_computation.4 | async-start | bytes 2293760
  11.2 1.1 copy-start.2
  12.4 1.1 copy-start.3
  13.5 1.1 copy-start.4
  99.4 2.7 copy-start
  102.1 2.7 copy-start.5
  104.8 2.6 copy-start.6
  107.4 5.6 %copy-start.1 = (bf16[8,448,896]{2,1,0:T(8,128)(2,1)S(1)}, bf16[8,448,896]{2,1,0:T(8,128)(2,1)}, u32[]{:S(2)}) copy-start(bf16[8,448,896]{2,1,0:T(8,128)(2,1)} %copy-done) | copy-start | bytes 19267588
  107.4 5.7 %copy-start.11 = (bf16[256,3584]{1,0:T(8,128)(2,1)S(1)}, bf16[256,3584]{1,0:T(8,128)(2,1)}, u32[]{:S(2)}) copy-start(bf16[256,3584]{1,0:T(8,128)(2,1)} %all-gather.3.cloned.1.call-done) | copy-start | bytes 5505028
  113.0 3.2 copy-start.15
  113.1 3.8 %copy-start.7 = (bf16[8,448,896]{2,1,0:T(8,128)(2,1)S(1)}, bf16[8,448,896]{2,1,0:T(8,128)(2,1)}, u32[]{:S(2)}) copy-start(bf16[8,448,896]{2,1,0:T(8,128)(2,1)} %copy-done.6) | copy-start | bytes 19267588
  116.1 0.8 copy-start.12
  116.9 3.5 %copy-start.14 = (f32[1,3584]{1,0:T(1,128)S(1)}, f32[1,3584]{1,0:T(1,128)}, u32[]{:S(2)}) copy-start(f32[1,3584]{1,0:T(1,128)} %param.10) | copy-start | bytes 43012
  120.3 42.2 %copy-start.10 = (bf16[64,3584]{1,0:T(8,128)(2,1)S(1)}, bf16[64,3584]{1,0:T(8,128)(2,1)}, u32[]{:S(2)}) copy-start(bf16[64,3584]{1,0:T(8,128)(2,1)} %param.8) | copy-start | bytes 1376260
  120.3 83.6 %all-gather.5.cloned.1.call-start = ((), (), s32[]{:S(2)}) async-start(), calls=%async_computation.3 | async-start | bytes 2293760 | tf_op jit(solution)/shard_map/all_gather | solution.py:374
  162.9 52.7 %slice-start = ((s8[6422528]{0:T(1024)(128)(4,1)}), s8[2228224]{0:T(1024)(128)(4,1)S(1)}, s32[]{:S(2)}) async-start(s8[6422528]{0:T(1024)(128)(4,1)} %bitcast.44), calls=%async_computation.6 | async-start | bytes 4456448
  163.9 163.9 %reduce-scatter.9.cloned.1.call-start = ((), (), s32[]{:S(2)}) async-start(), calls=%async_computation.5 | async-start | bytes 2293760 | tf_op jit(solution)/shard_map/reduce_scatter | solution.py:379
  203.9 11.6 %slice-start.1 = ((s8[6422528]{0:T(1024)(128)(4,1)}), s8[4194304]{0:T(1024)(128)(4,1)S(1)}, s32[]{:S(2)}) async-start(s8[6422528]{0:T(1024)(128)(4,1)} %bitcast.44), calls=%async_computation.7 | async-start | bytes 8388608
  210.4 5.1 %copy-start.13 = (bf16[256,896]{1,0:T(8,128)(2,1)}, bf16[256,896]{1,0:T(8,128)(2,1)S(1)}, u32[]{:S(2)}) copy-start(bf16[256,896]{1,0:T(8,128)(2,1)S(1)} %get-tuple-element.18) | copy-start | bytes 1376260
  225.6 2.6 copy-start.8
  324.7 3.2 copy-start.9
Sparse Core Ops, SparseCore 0:
  11.3 43.8 all-gather.2
  120.4 40.0 reduce-scatter.6
  164.1 39.8 all-gather.4
  219.0 38.9 reduce-scatter.8

commit v2 on v1

--- a/solution.py
+++ b/solution.py
@@ -141,7 +141,7 @@
             pltpu.SemaphoreType.DMA((count, 2 * outer)),
         ],
         compiler_params=pltpu.CompilerParams(
-            collective_id=0, has_side_effects=True, vmem_limit_bytes=8 * 1024 * 1024
+            collective_id=0, has_side_effects=True, vmem_limit_bytes=VMEM_LIMIT
         ),
         cost_estimate=pl.CostEstimate(
             flops=200_000_000, bytes_accessed=2 * parts * size, transcendentals=0
@@ -338,6 +338,187 @@
     )(left, right)
 
 
+def middle_kernel(span, chunks, partial, carried, post, out, from_left, from_right,
+                  right_send, right_recv, left_send, left_recv,
+                  gather_right, gather_left, gather_recv):
+    t = lax.axis_index("tp")
+    rows, width = carried.shape
+    piece = rows // chunks
+    last = span - 1
+
+    def hop(src, dst, send_sem, recv_sem, target):
+        return pltpu.make_async_remote_copy(
+            src_ref=src,
+            dst_ref=dst,
+            send_sem=send_sem,
+            recv_sem=recv_sem,
+            device_id={"tp": target},
+            device_id_type=MESH,
+        )
+
+    def right_hop(k, o):
+        spot = from_left.at[k, o]
+        return hop(spot, spot, right_send.at[k, o], right_recv.at[k, o], t + 1)
+
+    def left_hop(k, o):
+        spot = from_right.at[k, o]
+        return hop(spot, spot, left_send.at[k, o], left_recv.at[k, o], t - 1)
+
+    def block(o, k):
+        return pl.ds(pl.multiple_of(o * rows + k * piece, 16), piece)
+
+    def gather_hop(k, o, sem, target):
+        spot = out.at[block(o, k)]
+        return hop(spot, spot, sem, gather_recv.at[k, o], target)
+
+    barrier = pltpu.get_barrier_semaphore()
+
+    @pl.when(t > 0)
+    def _():
+        pl.semaphore_signal(barrier, inc=1, device_id={"tp": t - 1}, device_id_type=MESH)
+
+    @pl.when(t < last)
+    def _():
+        pl.semaphore_signal(barrier, inc=1, device_id={"tp": t + 1}, device_id_type=MESH)
+
+    @pl.when((t > 0) & (t < last))
+    def _():
+        pl.semaphore_wait(barrier, 2)
+
+    @pl.when((t == 0) | (t == last))
+    def _():
+        pl.semaphore_wait(barrier, 1)
+
+    def add_into(ref, k, o):
+        ref[k, o] = (
+            ref[k, o].astype(jnp.float32) + partial[block(o, k), :].astype(jnp.float32)
+        ).astype(ref.dtype)
+
+    def pass_on(k):
+        for i in range(last):
+            o = last - i
+
+            @pl.when(t == 0)
+            def _():
+                from_left[k, o] = partial[block(o, k), :]
+                right_hop(k, o).start()
+
+            @pl.when((t > 0) & (t < o))
+            def _():
+                right_hop(k, o).wait_recv()
+                add_into(from_left, k, o)
+                right_hop(k, o).start()
+
+            @pl.when(t == last)
+            def _():
+                from_right[k, i] = partial[block(i, k), :]
+                left_hop(k, i).start()
+
+            @pl.when((t < last) & (t > i))
+            def _():
+                left_hop(k, i).wait_recv()
+                add_into(from_right, k, i)
+                left_hop(k, i).start()
+
+    def settle(k):
+        @pl.when(t > 0)
+        def _():
+            right_hop(k, t).wait_recv()
+
+        @pl.when(t == 0)
+        def _():
+            from_left[k, 0] = jnp.zeros_like(from_left[k, 0])
+
+        @pl.when(t < last)
+        def _():
+            left_hop(k, t).wait_recv()
+
+        @pl.when(t == last)
+        def _():
+            from_right[k, last] = jnp.zeros_like(from_right[k, last])
+
+        whole = partial[block(t, k), :].astype(jnp.float32)
+        whole = whole + from_left[k, t].astype(jnp.float32)
+        whole = whole + from_right[k, t].astype(jnp.float32)
+        whole = whole.astype(jnp.bfloat16).astype(jnp.float32)
+        factor = rms_factor(whole)
+        delta = carried[pl.ds(k * piece, piece), :] * post[...]
+        out[block(t, k), :] = norm_back(delta, whole * factor, factor).astype(out.dtype)
+
+        @pl.when(t < last)
+        def _():
+            gather_hop(k, t, gather_right.at[k, t], t + 1).start()
+
+        @pl.when(t > 0)
+        def _():
+            gather_hop(k, t, gather_left.at[k, t], t - 1).start()
+
+    def spread(k):
+        for i in range(span):
+            o = last - i
+
+            @pl.when(o < t)
+            def _():
+                gather_hop(k, o, gather_right.at[k, o], t - 1).wait_recv()
+
+                @pl.when(t < last)
+                def _():
+                    gather_hop(k, o, gather_right.at[k, o], t + 1).start()
+
+            @pl.when(i > t)
+            def _():
+                gather_hop(k, i, gather_left.at[k, i], t + 1).wait_recv()
+
+                @pl.when(t > 0)
+                def _():
+                    gather_hop(k, i, gather_left.at[k, i], t - 1).start()
+
+    for step in range(chunks + 2):
+        if step < chunks:
+            pass_on(step)
+        if 0 <= step - 1 < chunks:
+            settle(step - 1)
+        if 0 <= step - 2:
+            spread(step - 2)
+    for k in range(chunks):
+        for o in range(span):
+
+            @pl.when(t < o)
+            def _():
+                right_hop(k, o).wait_send()
+
+            @pl.when(t > o)
+            def _():
+                left_hop(k, o).wait_send()
+
+            @pl.when((o <= t) & (t < last))
+            def _():
+                gather_hop(k, o, gather_right.at[k, o], t + 1).wait_send()
+
+            @pl.when((o >= t) & (t > 0))
+            def _():
+                gather_hop(k, o, gather_left.at[k, o], t - 1).wait_send()
+
+
+def middle_exchange(partial, carried, post, span):
+    rows, width = carried.shape
+    chunks = 4 if rows % 64 == 0 else 1
+    slots = pltpu.VMEM((chunks, span, rows // chunks, width), jnp.bfloat16)
+    return pl.pallas_call(
+        functools.partial(middle_kernel, span, chunks),
+        out_shape=jax.ShapeDtypeStruct(partial.shape, jnp.bfloat16),
+        in_specs=[pl.BlockSpec(memory_space=pltpu.VMEM)] * 3,
+        out_specs=pl.BlockSpec(memory_space=pltpu.VMEM),
+        scratch_shapes=[slots, slots] + [pltpu.SemaphoreType.DMA((chunks, span))] * 7,
+        compiler_params=pltpu.CompilerParams(
+            collective_id=2, has_side_effects=True, vmem_limit_bytes=32 * 1024 * 1024
+        ),
+        cost_estimate=pl.CostEstimate(
+            flops=200_000_000, bytes_accessed=4 * partial.size, transcendentals=0
+        ),
+    )(partial, carried, post)
+
+
 def body(parts, layer_inputs, out_grad, pre_scale, post_scale, gate_weight, up_weight, down_weight):
     tok_rows = out_grad.shape[0]
     layer_count = layer_inputs.shape[0]
@@ -363,15 +544,12 @@
         active, gelu_back = jax.vjp(gelu_tanh, gate_pre)
         hidden = (active * up_pre).astype(jnp.bfloat16)
         partial_mlp = nt(hidden, full_down)
-        mlp_out = lax.psum_scatter(
-            partial_mlp.astype(jnp.bfloat16), "tp", scatter_dimension=0, tiled=True
-        ).astype(jnp.float32)
-        mlp_out = lax.optimization_barrier(mlp_out.astype(jnp.bfloat16)).astype(jnp.float32)
-        second_rms = rms_factor(mlp_out)
-        mlp_grad = norm_back(
-            carried * post_scale[layer_id], mlp_out * second_rms, second_rms
-        ).astype(jnp.bfloat16)
-        grad_group = lax.all_gather(mlp_grad, "tp", axis=0, tiled=True)
+        grad_group = middle_exchange(
+            partial_mlp.astype(jnp.bfloat16),
+            carried,
+            post_scale[layer_id][None],
+            lax.axis_size("tp"),
+        )
         hidden_grad = jnp.dot(grad_group, full_down, preferred_element_type=jnp.float32)
         gate_delta = gelu_back(hidden_grad * up_pre)[0].astype(jnp.bfloat16)
         up_delta = (hidden_grad * active).astype(jnp.bfloat16)

time: 339 us -> 329 us (0.971)
  Pallas kernels: 179 us -> 274 us
  waiting for transfers between devices: 79.9 us -> 0.06 us
  local copies, waits for them, and re-layouts: 23.9 us -> 10.9 us
  matrix products: 26.9 us -> 17.8 us
    pallas_call x0 -> x1, Pallas kernels: none -> 94.9 us  [middle_exchange(): pl.pallas_call(functools.partial(middle_kernel, span, chunks), out_shape=...]
    unnamed x5 -> x2, waiting for transfers between devices: 40.2 us -> 0.03 us
    all_gather x1 -> x0, waiting for transfers between devices: 39.7 us -> none  [body(): grad_group = lax.all_gather(mlp_grad, 'tp', axis=0, tiled=True)]
    unnamed x37 -> x20, local copies, waits for them, and re-layouts: 13.8 us -> 1.51 us
    dot_general x3, matrix products: 11.8 us -> 7.5 us  [nt(): lax.dot_general(x, y, (((1,), (1,)), ((), ())), preferred_element_type=jn...]
    dot_general x1, matrix products: 6.49 us -> 2.57 us  [body(): jnp.dot(grad_group, full_down, preferred_element_type=jnp.float32)]
    all_gather x1 -> x0, local copies, waits for them, and re-layouts: 3.8 us -> none  [body(): grad_group = lax.all_gather(mlp_grad, 'tp', axis=0, tiled=True)]
  transfers between devices with their start and end apart: 4 -> 2, of which waited for: 2 -> 0; matrix products, arithmetic and copies ran while one was open for 4% -> 4% of each run, Pallas kernels for 53% -> 54%
where the time goes in v2:
time: 329 us
  Pallas kernels  274 us (83%)
  matrix products  17.8 us (5%)
  between operations  14.2 us (4%)
  other arithmetic  11.9 us (4%)
  local copies, waits for them, and re-layouts  10.9 us (3%)
    pallas_call x1, Pallas kernels, middle_exchange(): pl.pallas_call(functools.partial(middle_kernel, span, chunks), out_shape=...  94.9 us
    pallas_call x1, Pallas kernels, scatter_products(): pl.pallas_call(functools.partial(scatter_kernel, outer, scale), out_shape...  93.4 us
    pallas_call x1, Pallas kernels, gather_blocks(): pl.pallas_call(functools.partial(gather_kernel, outer, count), out_shape=...  85.4 us
    dot_general x3, matrix products, nt(): lax.dot_general(x, y, (((1,), (1,)), ((), ())), preferred_element_type=jn...  7.5 us
  transfers between devices with their start and end apart: 2, of which 0 were waited for; matrix products, arithmetic and copies ran while one was open for 4% of the time, Pallas kernels for 54%

profile of v2, /device:TPU:0, one launch (start us, length us, event | category | flops | bytes accessed | tf_op | source)
XLA Modules:
  0.0 328.8 jit_solution(14358962494997750171)
XLA Ops:
  7.2 0.0 all-gather.2.cloned.1.call-start
  7.2 1.2 fusion.10
  8.4 0.8 reduce
  9.2 2.0 fusion.4
  11.2 0.0 all-gather.2.cloned.1.call-update
  11.2 0.0 reduce-scatter.4.cloned.1.call-start
  11.2 1.1 convert_element_type.33.carried
  12.3 85.4 %shard_map.102 = (bf16[8,448,896]{2,1,0:T(8,128)(2,1)}, bf16[8,448,896]{2,1,0:T(8,128)(2,1)}, bf16[8,448,896]{2,1,0:T(8,128)(2,1)}) custom-call(bf16[448,896]{1,0:T(8,128)(2,1)} %bitcast.47, bf16[448,896]{1,0:T(8,128)(2,1)} %bitcast.48, bf16[448,896]{1,0:T(8,128)(2,1)} %bitcast.49), custom_call_target="tpu_custom_call" | custom-call | flops 200000000 | bytes 38535168 | tf_op jit(solution)/shard_map/pallas_call | solution.py:131
  97.8 0.0 all-gather.2.cloned.1.call-done
  97.8 0.0 copy-start.4
  97.8 0.0 copy-start.5
  97.8 5.6 %fusion.18 = f32[256,896]{1,0:T(8,128)S(1)} fusion(bf16[256,3584]{1,0:T(8,128)(2,1)} %all-gather.2.cloned.1.call-done, bf16[3584,896]{1,0:T(8,128)(2,1)} %bitcast.52), kind=kOutput, calls=%fused_computation.33 | convolution fusion | flops 1644167168 | bytes 9175040 | tf_op jit(solution)/shard_map/dot_general | solution.py:542
  103.4 0.0 copy-done.4
  103.4 0.1 copy-done.5
  103.5 0.0 copy-start.7
  103.5 2.1 multiply_convert_fusion.1
  105.6 0.7 copy-done.7
  106.3 0.0 copy-start
  106.3 2.1 convolution_convert_fusion.partial
  108.4 0.0 copy-done
  108.5 0.0 slice-start
  108.5 94.9 %shard_map.103 = bf16[256,3584]{1,0:T(8,128)(2,1)S(1)} custom-call(bf16[256,3584]{1,0:T(8,128)(2,1)S(1)} %convolution_convert_fusion.partial, f32[64,3584]{1,0:T(8,128)S(1)} %convert_element_type.33.carried, f32[1,3584]{1,0:T(1,128)S(1)} %copy-done), custom_call_target="tpu_custom_call" | custom-call | flops 200000000 | bytes 3670016 | tf_op jit(solution)/shard_map/pallas_call | solution.py:507
  203.4 0.0 slice-start.1
  203.4 2.6 multiply_convert_fusion
  206.0 0.0 slice-done
  206.0 0.0 slice-done.1
  206.0 2.1 fusion.19
  208.1 3.3 %fusion = bf16[256,3584]{1,0:T(8,128)(2,1)} fusion(f32[256,3584]{1,0:T(8,128)S(1)} %fusion.19, bf16[256,896]{1,0:T(8,128)(2,1)S(1)} %get-tuple-element.17, bf16[3584,896]{1,0:T(8,128)(2,1)S(1)} %bitcast.45), kind=kOutput, calls=%fused_computation.1 | convolution fusion | flops 1646002176 | bytes 12386304 | tf_op jit(solution)/shard_map/dot_general | solution.py:532
  211.4 0.0 reduce-scatter.4.cloned.1.call-update
  211.5 2.3 copy.21
  213.8 0.0 copy-start.1
  213.8 3.9 %copy.20 = bf16[256,3584]{0,1:T(8,128)(2,1)} copy(bf16[256,3584]{1,0:T(8,128)(2,1)} %all-gather.2.cloned.1.call-done) | data formatting | bytes 3670016 | tf_op jit(solution)/shard_map/all_gather | solution.py:538
  217.7 0.0 copy-start.2
  217.7 1.3 pad_maximum_fusion.1.right
  219.0 0.0 copy-done.1
  219.0 0.7 copy-done.2
  219.7 2.1 pad_maximum_fusion.left
  221.8 93.4 %shard_map.104 = bf16[3,448,896]{2,1,0:T(8,128)(2,1)} custom-call(bf16[2,3584,256]{2,1,0:T(8,128)(2,1)} %pad_maximum_fusion.left, bf16[3,256,896]{2,1,0:T(8,128)(2,1)} %pad_maximum_fusion.1.right), custom_call_target="tpu_custom_call" | custom-call | flops 4932501504 | bytes 19267584 | tf_op jit(solution)/shard_map/pallas_call | solution.py:312
  315.3 0.0 copy-start.3
  315.3 0.0 copy-start.6
  315.3 3.2 slice_bitcast_fusion
  318.5 0.0 reduce-scatter.4.cloned.1.call-done
  318.5 0.0 copy-done.3
  318.5 1.3 fusion.5
  319.8 0.0 copy-done.6
  319.8 2.1 fusion.9
  (3 shorter events, 0.0 us)
Async XLA Ops:
  7.2 90.6 %all-gather.2.cloned.1.call-start = ((), (), s32[]{:S(2)}) async-start(), calls=%async_computation.1 | async-start | bytes 2293760 | tf_op jit(solution)/shard_map/all_gather | solution.py:538
  11.2 307.3 %reduce-scatter.4.cloned.1.call-start = ((), (), s32[]{:S(2)}) async-start(), calls=%async_computation.2 | async-start | bytes 2293760 | tf_op jit(solution)/shard_map/reduce_scatter | solution.py:557
  97.8 5.6 %copy-start.4 = (bf16[8,448,896]{2,1,0:T(8,128)(2,1)S(1)}, bf16[8,448,896]{2,1,0:T(8,128)(2,1)}, u32[]{:S(2)}) copy-start(bf16[8,448,896]{2,1,0:T(8,128)(2,1)} %get-tuple-element.8) | copy-start | bytes 19267588
  97.8 5.7 %copy-start.5 = (bf16[256,3584]{1,0:T(8,128)(2,1)S(1)}, bf16[256,3584]{1,0:T(8,128)(2,1)}, u32[]{:S(2)}) copy-start(bf16[256,3584]{1,0:T(8,128)(2,1)} %all-gather.2.cloned.1.call-done) | copy-start | bytes 5505028
  103.5 2.8 copy-start.7
  106.3 2.1 copy-start
  108.5 97.5 %slice-start = ((s8[6422528]{0:T(1024)(128)(4,1)}), s8[4194304]{0:T(1024)(128)(4,1)S(1)}, s32[]{:S(2)}) async-start(s8[6422528]{0:T(1024)(128)(4,1)} %bitcast.53), calls=%async_computation.3 | async-start | bytes 8388608
  203.4 2.6 slice-start.1
  213.8 5.3 %copy-start.1 = (bf16[256,3584]{0,1:T(8,128)(2,1)S(1)}, bf16[256,3584]{0,1:T(8,128)(2,1)}, u32[]{:S(2)}) copy-start(bf16[256,3584]{0,1:T(8,128)(2,1)} %copy.21) | copy-start | bytes 5505028
  217.7 2.0 copy-start.2
  315.3 3.2 copy-start.3
  315.3 4.5 %copy-start.6 = (bf16[64,3584]{1,0:T(8,128)(2,1)S(1)}, bf16[64,3584]{1,0:T(8,128)(2,1)}, u32[]{:S(2)}) copy-start(bf16[64,3584]{1,0:T(8,128)(2,1)} %param.8) | copy-start | bytes 1376260
Sparse Core Ops, SparseCore 0:
  11.3 43.8 all-gather.1
  211.6 37.0 reduce-scatter.3
